TPU v7x, 256 devices: a whole 4x4x8 slice. The times are simulated.
256 devices in a mesh: row: 16 (over z, core), col: 16 (over x, y).
Axes of the slice: x: 4, y: 4, z: 8, core: 2. Of those that a mesh axis runs over, the one named last changes fastest.
Arguments:
- genotypes: int32 [4096, 16384], P(('row', 'col')), may hold values from 0 to 2, as said below
- snp_index: int32 [4096], P(('row', 'col')), may hold values from 0 to 16383, as said below
- freq_table: float32 [16384], replicated, as said below
- prior: float32 [16384, 16384], P('row', 'col'), as said below
- start_vectors: float32 [16384, 20], P('row'), may hold values from -6 to 6
Outputs:
- grm: float32 [16384, 16384], P('row', 'col')
- pcs: float32 [16384, 20], P('col')
- spectrum: float32 [3, 20], replicated
Inputs may be any that keep to these rules, and one draw needn't show every extreme that they name: `genotypes`: genotype dosages 0, 1 or 2. `snp_index`: strictly increasing; entry j lies in 4 * j to 4 * j + 3. `freq_table`: frequencies are multiples of 1/1024 between 52/1024 and 512/1024. `prior`: exactly symmetric; diagonal between 1 and 2, off-diagonal entries small.
All inputs are finite; a program needn't handle non-finite values.
Results may differ from a plain program's by a relative error of at most 0.0075.
Values may be sent and summed in bfloat16 or wider, within the bound.
No kernel may reach another device: no remote copies, remote signals or barrier semaphores. Data moves between devices by JAX's collectives and lax.ppermute only.
A program may use at most 128 MiB of HBM per device.

v0:
```python
import jax
import jax.numpy as jnp
from jax import lax
from jax.sharding import Mesh
from jax.sharding import PartitionSpec as P

S = 16384
ITERS = 3
COL = ("col_0", "col_1")
ROW_COL = ("row", "col_0", "col_1")


def total_of_pieces(array, axis):
    return lax.all_gather(array, axis).sum(0)


def copy_for_each(array, axis):
    length = lax.axis_size(axis)
    return lax.all_to_all(
        jnp.broadcast_to(array[None], (length, *array.shape)), axis, 0, 0, tiled=True
    )


def taken_together(array, axis):
    return copy_for_each(array, axis).sum(axis=0)


def in_one(arrays, axis):
    ravelled, at, outs = (jnp.concatenate([a.reshape(-1) for a in arrays]), 0, [])
    so_far = taken_together(ravelled, axis)
    for a in arrays:
        outs.append(so_far[at : at + a.size].reshape(a.shape))
        at += a.size
    return tuple(outs)


def one_axis_at_a_time(array, axes):
    for axis in axes:
        array = lax.psum(array, axis)
    return array


def standardize(genotypes, allele_freq):
    doubled = 2.0 * allele_freq
    spread = jnp.sqrt(doubled * (1.0 - allele_freq))
    return (genotypes.astype(jnp.float32) - doubled[:, None]) / spread[:, None]


def orthonormal(factor, image):
    return lax.linalg.triangular_solve(factor, image, left_side=False, lower=True, transpose_a=True)


def apply_tile(tile, vectors, transposed):
    if transposed:
        return lax.dot_general(tile, vectors, (((0,), (0,)), ((), ())))
    return jnp.dot(tile, vectors)


def local_gram(image):
    return jnp.dot(image.T, image)


def body(genotypes, snp_index, freq_table, prior, start_vectors):
    allele_freq = jnp.take(freq_table, snp_index)
    standard = standardize(genotypes, allele_freq).astype(jnp.bfloat16)
    row_count = lax.axis_size("row")
    col_count = lax.axis_size(COL)
    own_snps = genotypes.shape[0]
    total_snps = own_snps * row_count * col_count
    row_piece = lax.all_to_all(standard, "row", split_axis=1, concat_axis=0, tiled=True)
    col_piece = lax.all_to_all(standard, COL, split_axis=1, concat_axis=0, tiled=True)
    col_piece = col_piece.reshape(col_count, 1, own_snps, col_piece.shape[1])
    col_panel = lax.all_gather(col_piece, "row", axis=1, tiled=True)
    col_panel = col_panel.reshape(total_snps, col_panel.shape[3])
    window = lax.dot_general(
        lax.all_gather(row_piece, COL, axis=0, tiled=True),
        col_panel,
        (((0,), (0,)), ((), ())),
        preferred_element_type=jnp.float32,
    )
    grm = prior + window / total_snps
    scaled_start = start_vectors / jnp.sqrt(jnp.float32(S))
    diagonals = []
    image = total_of_pieces(apply_tile(grm, scaled_start, True), "row")
    for step in range(1, ITERS):
        if step % 2 == 1:
            product, gram = in_one((apply_tile(grm, image, False), local_gram(image)), COL)
        else:
            product, gram = (
                total_of_pieces(apply_tile(grm, image, True), "row"),
                total_of_pieces(local_gram(image), "row"),
            )
        factor = jnp.linalg.cholesky(gram)
        diagonals.append(jnp.diagonal(factor))
        image = orthonormal(factor, product)
    gram = one_axis_at_a_time(local_gram(image), COL)
    factor = jnp.linalg.cholesky(gram)
    diagonals.append(jnp.diagonal(factor))
    vectors = orthonormal(factor, image)
    pcs = vectors * jnp.sqrt(jnp.float32(S))
    spectrum = jnp.stack(diagonals, axis=0)
    return (grm, pcs, spectrum)


def solution(mesh):
    finer = Mesh(mesh.devices.reshape(mesh.shape["row"], 4, 4), ("row", "col_0", "col_1"))
    in_specs = (P(ROW_COL, None), P(ROW_COL), P(), P("row", COL), P("row", None))
    out_specs = (P("row", COL), P(COL, None), P())
    return jax.shard_map(body, mesh=finer, in_specs=in_specs, out_specs=out_specs, check_vma=False)
```

profile of v0, /device:TPU:32, one launch (start us, length us, event | category | flops | bytes accessed | tf_op | source)
XLA Modules:
  0.0 351.4 jit_solution(14662210511644327606)
XLA Ops:
  7.2 0.7 compare_select_fusion
  8.0 0.7 gather_fusion
  8.7 0.7 broadcast_multiply_fusion
  9.3 1.4 divide_convert_fusion
  10.8 18.3 %all_to_all.38 = bf16[16,16,1024]{2,0,1:T(8,128)(2,1)S(1)} all-to-all(bf16[16,16,1024]{2,0,1:T(8,128)(2,1)S(1)} %bitcast.82), channel_id=1, replica_groups=mesh['row'=16,'col_0'=4,'col_1'=4] {'col_0','col_1'}, dimensions={1} | all-to-all | bytes 1048576 | tf_op jit(solution)/shard_map/all_to_all | solution.py:71
  29.1 1.1 copy.44
  30.3 25.6 %all_to_all.39 = bf16[16,16,1024]{2,0,1:T(8,128)(2,1)} all-to-all(bf16[16,16,1024]{2,0,1:T(8,128)(2,1)S(1)} %bitcast.83), channel_id=1, replica_groups=mesh['row'=16,'col_0'=4,'col_1'=4] {'row'}, dimensions={1} | all-to-all | bytes 1048576 | tf_op jit(solution)/shard_map/all_to_all | solution.py:70
  55.9 37.5 %all-gather.12.cloned.1.call-done = bf16[16,256,1024]{2,0,1:T(8,128)(2,1)} async-done(((bf16[16,16,1024]{2,0,1:T(8,128)(2,1)}), bf16[16,256,1024]{2,0,1:T(8,128)(2,1)}) %all-gather.12.cloned.1.call-update) | async-done | bytes 8388624 | tf_op jit(solution)/shard_map/all_gather | solution.py:73
  93.5 11.3 %copy.45 = bf16[16,256,1024]{2,1,0:T(8,128)(2,1)} copy(bf16[16,256,1024]{2,0,1:T(8,128)(2,1)} %all-gather.12.cloned.1.call-done) | data formatting | bytes 16777216 | tf_op jit(solution)/shard_map/all_gather | solution.py:73
  104.8 63.9 %all-gather.10.cloned.1.call-done = bf16[4096,1024]{1,0:T(8,128)(2,1)} async-done(((bf16[256,1024]{1,0:T(8,128)(2,1)}), bf16[4096,1024]{1,0:T(8,128)(2,1)}) %all-gather.10.cloned.1.call-update) | async-done | bytes 8388624 | tf_op jit(solution)/shard_map/all_gather | solution.py:76
  168.6 14.4 %multiply_add_fusion = f32[1024,1024]{1,0:T(8,128)S(1)} fusion(f32[1024,1024]{1,0:T(8,128)} %param.11, bf16[4096,1024]{1,0:T(8,128)(2,1)} %all-gather.10.cloned.1.call-done, bf16[4096,1024]{1,0:T(8,128)(2,1)} %bitcast.79), kind=kOutput, calls=%fused_computation.4 | convolution fusion | flops 8592031744 | bytes 25165824 | tf_op jit(solution)/shard_map/dot_general | solution.py:75
  183.0 2.0 copy-done.1
  185.0 1.0 fusion.1
  186.3 38.1 %all-gather.14.cloned.1.call-done = f32[16384,20]{0,1:T(8,128)} async-done(((f32[1024,20]{0,1:T(8,128)}), f32[16384,20]{0,1:T(8,128)}) %all-gather.14.cloned.1.call-update) | async-done | bytes 1310736 | tf_op jit(solution)/shard_map/all_gather | solution.py:14
  224.4 2.5 copy.58
  226.9 0.2 bitcast_reduce_fusion.1
  227.1 0.7 fusion.25
  228.0 0.4 reshape.79
  228.5 0.7 broadcast_in_dim.22
  229.2 27.1 %all_to_all.40 = f32[16,1,20880]{2,1,0:T(1,128)S(1)} all-to-all(f32[16,1,20880]{2,1,0:T(1,128)S(1)} %broadcast_in_dim.22), channel_id=1, replica_groups=mesh['row'=16,'col_0'=4,'col_1'=4] {'col_0','col_1'}, dimensions={0} | all-to-all | bytes 2672640 | tf_op jit(solution)/shard_map/all_to_all | solution.py:19
  256.3 0.8 reduce_sum.37
  257.3 1.8 cholesky.59
  259.2 0.6 compare_reduce_fusion.2
  259.8 0.7 fusion.16
  260.5 1.5 custom-call.13
  262.0 0.6 reshape.82
  262.6 0.6 convolution_bitcast_fusion.2
  263.2 3.2 fusion.27
  266.6 15.7 %all-gather.4 = f32[16,20,20]{2,1,0:T(8,128)S(1)} all-gather(f32[1,20,20]{2,1,0:T(8,128)S(1)} %convolution_bitcast_fusion.3), channel_id=4, replica_groups=mesh['row'=16,'col_0'=4,'col_1'=4] {'row'}, dimensions={0}, use_global_device_ids=true | all-gather | bytes 27200 | tf_op jit(solution)/shard_map/all_gather | solution.py:14
  282.4 1.8 cholesky.70
  284.3 0.6 compare_reduce_fusion.1
  284.9 0.7 fusion.15
  285.6 1.5 custom-call.14
  287.1 0.8 gather_fusion.2
  287.9 0.8 gather_fusion.1
  288.7 12.4 %all-gather.16.cloned.1.call-done = f32[16384,20]{0,1:T(8,128)} async-done(((f32[1024,20]{0,1:T(8,128)}), f32[16384,20]{0,1:T(8,128)}) %all-gather.16.cloned.1.call-update) | async-done | bytes 1310736 | tf_op jit(solution)/shard_map/all_gather | solution.py:14
  301.1 2.3 copy.59
  303.4 0.2 bitcast_reduce_fusion
  303.7 0.3 convolution_bitcast_fusion.1
  304.1 16.8 %psum.14 = f32[20,20]{0,1:T(8,128)S(1)} all-reduce(f32[20,20]{0,1:T(8,128)S(1)} %fusion.28), channel_id=1, replica_groups=mesh['row'=16,'col_0'=4,'col_1'=4] {'col_0'}, use_global_device_ids=true, to_apply=%region_6.9 | all-reduce | flops 400 | bytes 3200 | tf_op jit(solution)/shard_map/psum | solution.py:39
  320.9 16.8 %psum.15 = f32[20,20]{0,1:T(8,128)S(1)} all-reduce(f32[20,20]{0,1:T(8,128)S(1)} %psum.14), channel_id=1, replica_groups=mesh['row'=16,'col_0'=4,'col_1'=4] {'col_1'}, use_global_device_ids=true, to_apply=%region_7.10 | all-reduce | flops 400 | bytes 3200 | tf_op jit(solution)/shard_map/psum | solution.py:39
  337.8 1.8 cholesky.81
  339.7 0.6 compare_reduce_fusion
  340.3 0.7 select_bitcast_fusion
  341.0 0.8 gather_fusion.3
  341.8 1.5 custom-call.15
  343.3 1.0 fusion
  344.2 0.6 pad_maximum_fusion.1
  (37 shorter events, 1.6 us)
Async XLA Ops:
  7.2 0.8 copy-start
  7.2 86.3 %all-gather.12.cloned.1.call-start = ((), (), s32[]{:S(2)}) async-start(), calls=%async_computation.4 | async-start | bytes 8912896 | tf_op jit(solution)/shard_map/all_gather | solution.py:73
  30.2 138.4 %all-gather.10.cloned.1.call-start = ((), (), s32[]{:S(2)}) async-start(), calls=%async_computation.3 | async-start | bytes 8912896 | tf_op jit(solution)/shard_map/all_gather | solution.py:76
  55.9 168.6 %all-gather.14.cloned.1.call-start = ((), (), s32[]{:S(2)}) async-start(), calls=%async_computation.5 | async-start | bytes 1671168 | tf_op jit(solution)/shard_map/all_gather | solution.py:14
  168.6 16.4 %copy-start.3 = (f32[1024,20]{0,1:T(8,128)S(1)}, f32[1024,20]{0,1:T(8,128)}, u32[]{:S(2)}) copy-start(f32[1024,20]{0,1:T(8,128)} %param.12) | copy-start | bytes 245764
  183.0 2.0 copy-start.1
  186.1 115.0 %all-gather.16.cloned.1.call-start = ((), (), s32[]{:S(2)}) async-start(), calls=%async_computation.6 | async-start | bytes 1671168 | tf_op jit(solution)/shard_map/all_gather | solution.py:14
  224.4 2.7 copy-start.2
Sparse Core Ops, SparseCore 0:
  30.4 63.0 all-gather.11
  95.9 72.6 all-gather.9
  186.2 38.1 all-gather.13
  266.6 34.5 all-gather.15
where the time goes:
time: 352 us; the launch traced here: 351 us
  waiting for transfers between devices  152 us (43%)
  blocking collectives  120 us (34%)
  local copies, waits for them, and re-layouts  24.6 us (7%)
  matrix products  21.5 us (6%)
  other arithmetic  18.7 us (5%)
  between operations  13.9 us (4%)
    all_gather x1, waiting for transfers between devices, body(): lax.all_gather(row_piece, COL, axis=0, tiled=True)  63.9 us
    all_gather x2, waiting for transfers between devices, total_of_pieces(): return lax.all_gather(array, axis).sum(0)  50.5 us
    all_gather x1, waiting for transfers between devices, body(): col_panel = lax.all_gather(col_piece, 'row', axis=1, tiled=True)  37.5 us
    psum x2, blocking collectives, one_axis_at_a_time(): array = lax.psum(array, axis)  33.6 us
    all_to_all x1, blocking collectives, copy_for_each(): lax.all_to_all(jnp.broadcast_to(array[None], (length, *array.shape)), axi...  27.1 us
    all_to_all x1, blocking collectives, body(): lax.all_to_all(standard, 'row', split_axis=1, concat_axis=0, tiled=True)  25.6 us
    all_to_all x1, blocking collectives, body(): lax.all_to_all(standard, COL, split_axis=1, concat_axis=0, tiled=True)  18.3 us
    all_gather x1, blocking collectives, total_of_pieces(): return lax.all_gather(array, axis).sum(0)  15.7 us
  transfers between devices with their start and end apart: 4, of which 4 were waited for; matrix products, arithmetic and copies ran while one was open for 5% of the time, Pallas kernels for 0%

commit v1 on v0

--- a/solution.py
+++ b/solution.py
@@ -1,13 +1,31 @@
+import functools
 import jax
 import jax.numpy as jnp
 from jax import lax
 from jax.sharding import Mesh
 from jax.sharding import PartitionSpec as P
+from jax.lax import all_to_all, axis_size
 
 S = 16384
 ITERS = 3
 COL = ("col_0", "col_1")
 ROW_COL = ("row", "col_0", "col_1")
+
+
+def balance_map(chunk, axis_name, dim_at):
+    part_now = jnp.concatenate(
+        all_to_all(
+            jnp.stack([chunk for _ in range(axis_size(axis_name))]),
+            axis_name=axis_name,
+            split_axis=0,
+            concat_axis=0,
+        ),
+        axis=dim_at,
+    )
+    return part_now
+
+
+_start_scales = functools.partial(balance_map, axis_name="row", dim_at=1)
 
 
 def total_of_pieces(array, axis):
@@ -70,7 +88,7 @@
     row_piece = lax.all_to_all(standard, "row", split_axis=1, concat_axis=0, tiled=True)
     col_piece = lax.all_to_all(standard, COL, split_axis=1, concat_axis=0, tiled=True)
     col_piece = col_piece.reshape(col_count, 1, own_snps, col_piece.shape[1])
-    col_panel = lax.all_gather(col_piece, "row", axis=1, tiled=True)
+    col_panel = _start_scales(col_piece)
     col_panel = col_panel.reshape(total_snps, col_panel.shape[3])
     window = lax.dot_general(
         lax.all_gather(row_piece, COL, axis=0, tiled=True),

time: 352 us -> 434 us (1.23)
  waiting for transfers between devices: 152 us -> 230 us
  starting transfers between devices: 0.35 us -> 6.45 us
    all_to_all x0 -> x1, waiting for transfers between devices: none -> 181 us  [balance_map(): all_to_all(jnp.stack([chunk for _ in range(axis_size(axis_name))]), axis_...]
    all_gather x1, waiting for transfers between devices: 63.9 us -> 0.01 us  [body(): lax.all_gather(row_piece, COL, axis=0, tiled=True)]
    all_gather x1 -> x0, waiting for transfers between devices: 37.5 us -> none  [body(): col_panel = lax.all_gather(col_piece, 'row', axis=1, tiled=True)]
    all_gather x1 -> x0, local copies, waits for them, and re-layouts: 11.3 us -> none  [body(): col_panel = lax.all_gather(col_piece, 'row', axis=1, tiled=True)]
    all_to_all x1, local copies, waits for them, and re-layouts: 1.08 us -> 8.52 us  [balance_map(): all_to_all(jnp.stack([chunk for _ in range(axis_size(axis_name))]), axis_...]
    all_to_all x0 -> x1, starting transfers between devices: none -> 6.33 us  [balance_map(): all_to_all(jnp.stack([chunk for _ in range(axis_size(axis_name))]), axis_...]
  transfers between devices with their start and end apart: 4 -> 4, of which waited for: 4 -> 3; matrix products, arithmetic and copies ran while one was open for 5% -> 3% of each run, Pallas kernels for 0% -> 0%
where the time goes in v1:
time: 434 us; the launch traced here: 433 us
  waiting for transfers between devices  230 us (53%)
  blocking collectives  117 us (27%)
  local copies, waits for them, and re-layouts  25 us (6%)
  matrix products  21.5 us (5%)
  other arithmetic  18.8 us (4%)
  between operations  13.9 us (3%)
  starting transfers between devices  6.45 us (1%)
    all_to_all x1, waiting for transfers between devices, balance_map(): all_to_all(jnp.stack([chunk for _ in range(axis_size(axis_name))]), axis_...  181 us
    all_gather x2, waiting for transfers between devices, total_of_pieces(): return lax.all_gather(array, axis).sum(0)  48.2 us
    psum x2, blocking collectives, one_axis_at_a_time(): array = lax.psum(array, axis)  33.6 us
    all_to_all x1, blocking collectives, copy_for_each(): lax.all_to_all(jnp.broadcast_to(array[None], (length, *array.shape)), axi...  27.1 us
    all_to_all x1, blocking collectives, body(): lax.all_to_all(standard, 'row', split_axis=1, concat_axis=0, tiled=True)  22.7 us
    all_to_all x1, blocking collectives, body(): lax.all_to_all(standard, COL, split_axis=1, concat_axis=0, tiled=True)  18.3 us
    all_gather x1, blocking collectives, total_of_pieces(): return lax.all_gather(array, axis).sum(0)  15.7 us
    dot_general x1, matrix products, body(): lax.dot_general(lax.all_gather(row_piece, COL, axis=0, tiled=True), col_p...  14.4 us
  transfers between devices with their start and end apart: 4, of which 3 were waited for; matrix products, arithmetic and copies ran while one was open for 3% of the time, Pallas kernels for 0%

profile of v1, /device:TPU:32, one launch (start us, length us, event | category | flops | bytes accessed | tf_op | source)
XLA Modules:
  0.0 433.5 jit_solution(18113665832175026828)
XLA Ops:
  7.2 0.7 compare_select_fusion
  8.0 0.7 gather_fusion
  8.7 0.7 broadcast_multiply_fusion
  9.3 1.4 divide_convert_fusion
  10.8 18.3 %all_to_all.43 = bf16[16,16,1024]{2,0,1:T(8,128)(2,1)S(1)} all-to-all(bf16[16,16,1024]{2,0,1:T(8,128)(2,1)S(1)} %bitcast.84), channel_id=1, replica_groups=mesh['row'=16,'col_0'=4,'col_1'=4] {'col_0','col_1'}, dimensions={1} | all-to-all | bytes 1048576 | tf_op jit(solution)/shard_map/all_to_all | solution.py:89
  29.1 22.7 %all_to_all.44 = bf16[16,16,1024]{2,0,1:T(8,128)(2,1)} all-to-all(bf16[16,16,1024]{2,0,1:T(8,128)(2,1)S(1)} %bitcast.85), channel_id=1, replica_groups=mesh['row'=16,'col_0'=4,'col_1'=4] {'row'}, dimensions={1} | all-to-all | bytes 1048576 | tf_op jit(solution)/shard_map/all_to_all | solution.py:88
  51.8 4.3 stack.15
  56.2 6.3 %all-to-all-start.2 = ((bf16[16,16,1,16,1024]{4,3,1,2,0:T(8,128)(2,1)}), bf16[16,16,1,16,1024]{4,3,1,2,0:T(8,128)(2,1)}, u32[]{:S(2)}, u32[]{:S(2)}) async-start(bf16[16,16,1,16,1024]{4,3,1,2,0:T(8,128)(2,1)} %stack.15), calls=%async_computation.2 | async-start | bytes 16777216 | tf_op jit(solution)/shard_map/all_to_all | solution.py:17
  62.5 0.7 all-gather.8.cloned.1.call-update
  63.3 181.5 %all-to-all-done.2 = bf16[16,16,1,16,1024]{4,3,1,2,0:T(8,128)(2,1)} async-done(((bf16[16,16,1,16,1024]{4,3,1,2,0:T(8,128)(2,1)}), bf16[16,16,1,16,1024]{4,3,1,2,0:T(8,128)(2,1)}, u32[]{:S(2)}, u32[]{:S(2)}) %all-to-all-start.2) | async-done | bytes 8388640 | tf_op jit(solution)/shard_map/all_to_all | solution.py:17
  244.7 8.5 %copy.43 = bf16[16,16,1,16,1024]{4,3,0,1,2:T(8,128)(2,1)} copy(bf16[16,16,1,16,1024]{4,3,1,2,0:T(8,128)(2,1)} %all-to-all-done.2) | data formatting | bytes 16777216 | tf_op jit(solution)/shard_map/all_to_all | solution.py:17
  253.3 14.4 %multiply_add_fusion = f32[1024,1024]{1,0:T(8,128)S(1)} fusion(f32[1024,1024]{1,0:T(8,128)} %param.11, bf16[4096,1024]{1,0:T(8,128)(2,1)} %all-gather.8.cloned.1.call-done, bf16[4096,1024]{1,0:T(8,128)(2,1)} %bitcast.81), kind=kOutput, calls=%fused_computation.4 | convolution fusion | flops 8592031744 | bytes 25165824 | tf_op jit(solution)/shard_map/dot_general | solution.py:93
  267.7 2.0 copy-done.1
  269.7 1.0 fusion.1
  270.8 35.8 %all-gather.10.cloned.1.call-done = f32[16384,20]{0,1:T(8,128)} async-done(((f32[1024,20]{0,1:T(8,128)}), f32[16384,20]{0,1:T(8,128)}) %all-gather.10.cloned.1.call-update) | async-done | bytes 1310736 | tf_op jit(solution)/shard_map/all_gather | solution.py:32
  306.5 2.5 copy.56
  309.0 0.2 bitcast_reduce_fusion.1
  309.3 0.7 fusion.25
  310.1 0.4 reshape.77
  310.6 0.7 broadcast_in_dim.22
  311.3 27.1 %all_to_all.45 = f32[16,1,20880]{2,1,0:T(1,128)S(1)} all-to-all(f32[16,1,20880]{2,1,0:T(1,128)S(1)} %broadcast_in_dim.22), channel_id=1, replica_groups=mesh['row'=16,'col_0'=4,'col_1'=4] {'col_0','col_1'}, dimensions={0} | all-to-all | bytes 2672640 | tf_op jit(solution)/shard_map/all_to_all | solution.py:37
  338.4 0.8 reduce_sum.37
  339.5 1.8 cholesky.59
  341.3 0.6 compare_reduce_fusion.2
  342.0 0.7 fusion.16
  342.6 1.5 custom-call.13
  344.1 0.6 reshape.80
  344.7 0.6 convolution_bitcast_fusion.2
  345.3 3.2 fusion.27
  348.7 15.7 %all-gather.3 = f32[16,20,20]{2,1,0:T(8,128)S(1)} all-gather(f32[1,20,20]{2,1,0:T(8,128)S(1)} %convolution_bitcast_fusion.3), channel_id=3, replica_groups=mesh['row'=16,'col_0'=4,'col_1'=4] {'row'}, dimensions={0}, use_global_device_ids=true | all-gather | bytes 27200 | tf_op jit(solution)/shard_map/all_gather | solution.py:32
  364.6 1.8 cholesky.70
  366.4 0.6 compare_reduce_fusion.1
  367.1 0.7 fusion.15
  367.7 1.5 custom-call.14
  369.2 0.8 gather_fusion.2
  370.0 0.8 gather_fusion.1
  370.8 12.4 %all-gather.12.cloned.1.call-done = f32[16384,20]{0,1:T(8,128)} async-done(((f32[1024,20]{0,1:T(8,128)}), f32[16384,20]{0,1:T(8,128)}) %all-gather.12.cloned.1.call-update) | async-done | bytes 1310736 | tf_op jit(solution)/shard_map/all_gather | solution.py:32
  383.2 2.3 copy.57
  385.8 0.3 convolution_bitcast_fusion.1
  386.2 16.8 %psum.14 = f32[20,20]{0,1:T(8,128)S(1)} all-reduce(f32[20,20]{0,1:T(8,128)S(1)} %fusion.28), channel_id=1, replica_groups=mesh['row'=16,'col_0'=4,'col_1'=4] {'col_0'}, use_global_device_ids=true, to_apply=%region_6.9 | all-reduce | flops 400 | bytes 3200 | tf_op jit(solution)/shard_map/psum | solution.py:57
  403.0 16.8 %psum.15 = f32[20,20]{0,1:T(8,128)S(1)} all-reduce(f32[20,20]{0,1:T(8,128)S(1)} %psum.14), channel_id=1, replica_groups=mesh['row'=16,'col_0'=4,'col_1'=4] {'col_1'}, use_global_device_ids=true, to_apply=%region_7.10 | all-reduce | flops 400 | bytes 3200 | tf_op jit(solution)/shard_map/psum | solution.py:57
  419.9 1.8 cholesky.81
  421.8 0.6 compare_reduce_fusion
  422.4 0.7 select_bitcast_fusion
  423.1 0.8 gather_fusion.3
  423.9 1.5 custom-call.15
  425.4 1.0 fusion
  426.4 0.6 pad_maximum_fusion.1
  (36 shorter events, 1.6 us)
Async XLA Ops:
  7.2 0.8 copy-start
  56.2 188.6 %all-to-all-start.2 = ((bf16[16,16,1,16,1024]{4,3,1,2,0:T(8,128)(2,1)}), bf16[16,16,1,16,1024]{4,3,1,2,0:T(8,128)(2,1)}, u32[]{:S(2)}, u32[]{:S(2)}) async-start(bf16[16,16,1,16,1024]{4,3,1,2,0:T(8,128)(2,1)} %stack.15), calls=%async_computation.2 | async-start | bytes 16777216 | tf_op jit(solution)/shard_map/all_to_all | solution.py:17
  62.5 190.8 %all-gather.8.cloned.1.call-start = ((), (), s32[]{:S(2)}) async-start(), calls=%async_computation.4 | async-start | bytes 8912896 | tf_op jit(solution)/shard_map/all_gather | solution.py:94
  63.2 243.3 %all-gather.10.cloned.1.call-start = ((), (), s32[]{:S(2)}) async-start(), calls=%async_computation.5 | async-start | bytes 1671168 | tf_op jit(solution)/shard_map/all_gather | solution.py:32
  253.3 16.4 %copy-start.3 = (f32[1024,20]{0,1:T(8,128)S(1)}, f32[1024,20]{0,1:T(8,128)}, u32[]{:S(2)}) copy-start(f32[1024,20]{0,1:T(8,128)} %param.12) | copy-start | bytes 245764
  267.7 2.0 copy-start.1
  270.7 112.5 %all-gather.12.cloned.1.call-start = ((), (), s32[]{:S(2)}) async-start(), calls=%async_computation.6 | async-start | bytes 1671168 | tf_op jit(solution)/shard_map/all_gather | solution.py:32
  306.5 2.7 copy-start.2
Sparse Core Ops, SparseCore 0:
  65.7 73.5 all-gather.7
  270.8 35.6 all-gather.9
  348.7 34.5 all-gather.11
